TPU v7x, 32 devices: a whole 2x2x4 slice. The times are simulated.
32 devices in a mesh: dp: 8 (over y, x, core), seq: 4 (over z).
Axes of the slice: x: 2, y: 2, z: 4, core: 2. Of those that a mesh axis runs over, the one named last changes fastest.
Arguments:
- qkv: bfloat16 [16, 1024, 4608], P('dp', 'seq'), may hold values from -20.4 to 20.4
- gate: float32 [16, 3072], P('dp'), may hold values from 0.5 to 2.5
- cotangent: bfloat16 [16, 1024, 3072], P('dp', 'seq'), may hold values from -6 to 6
- out_weight: bfloat16 [1536, 3072], replicated, may hold values from -0.15625 to 0.15625
- clip_lengths: int32 [16], replicated, may hold values from 1 to 768, as said below
- text_lengths: int32 [16], replicated, may hold values from 1 to 256, as said below
- plan: int32 [8], replicated, may hold values from 0 to 7, as said below
Outputs:
- mixed: bfloat16 [16, 1024, 3072], P('dp', 'seq')
- gate_grad: float32 [16, 3072], P('dp')
- weight_grad: float32 [1536, 3072], P(None, ('dp', 'seq'))
- qkv_grad: bfloat16 [16, 1024, 4608], P('dp', 'seq')
Inputs may be any that keep to these rules, and one draw needn't show every extreme that they name: clip_lengths[c] counts the live video positions of source clip c = 2 g + s (group g, slot s); some clip has exactly 768. text_lengths[c] counts the live text positions of source clip c; some clip has exactly 256. plan is a permutation of 0 to 7: the second clip of group g becomes the second clip of group plan[g].
All inputs are finite; a program needn't handle non-finite values.
Results may differ from a plain program's by a relative error of at most 0.011.
Values may be sent and summed in bfloat16 or wider, within the bound.
A program may use at most 128 MiB of HBM per device.

v0:
```python
import math

import jax
import jax.numpy as jnp
from jax import lax
from jax.experimental import pallas as pl
from jax.experimental.pallas import tpu as pltpu
from jax.sharding import PartitionSpec as P

HD = 128
TXT = 256
BLOCK = 256
NEGATIVE = -1e30
LOG2E = math.log2(math.e)


def dot(left, right, left_dim, right_dim):
    return lax.dot_general(
        left, right, (((left_dim,), (right_dim,)), ((), ())), preferred_element_type=jnp.float32
    )


def live_places(places, text_len, video_len):
    return (places < text_len) | ((places >= TXT) & (places < TXT + video_len))


def fill_bias(bias_ref, text_len, video_len):
    places = lax.broadcasted_iota(jnp.int32, bias_ref.shape, 0)
    bias_ref[...] = jnp.where(live_places(places, text_len, video_len), 0.0, NEGATIVE)


def forward_kernel(lens_ref, q_ref, k_ref, v_ref, out_ref, lse_ref, bias_ref):
    text_len, video_len = lens_ref[0], lens_ref[1]
    seq_len = q_ref.shape[0]
    score_scale = HD ** (-0.5) * LOG2E

    @pl.when(pl.program_id(0) == 0)
    def _():
        fill_bias(bias_ref, text_len, video_len)

    for block in range(seq_len // BLOCK):
        rows = pl.ds(block * BLOCK, BLOCK)
        scores = dot(k_ref[...], q_ref[rows, :], 1, 1) * score_scale + bias_ref[...]
        peak = jnp.max(scores, axis=0, keepdims=True)
        total = jnp.sum(jnp.exp2(scores - peak), axis=0, keepdims=True)
        places = block * BLOCK + lax.broadcasted_iota(jnp.int32, (1, BLOCK), 1)
        log_total = jnp.where(
            live_places(places, text_len, video_len), peak + jnp.log2(total), -NEGATIVE
        )
        lse_ref[0, :, rows] = log_total
        probs_low = jnp.exp2(scores - log_total).astype(jnp.bfloat16)
        out_ref[rows, :] = dot(v_ref[...], probs_low, 0, 0).T.astype(jnp.bfloat16)


def backward_kernel(
    lens_ref, q_ref, k_ref, v_ref, out_ref, d_ref, lse_ref,
    dq_ref, dk_ref, dv_ref, bias_ref, dk_sum, dv_sum,
):
    text_len, video_len = lens_ref[0], lens_ref[1]
    seq_len = q_ref.shape[0]
    score_scale = HD ** (-0.5)

    @pl.when(pl.program_id(0) == 0)
    def _():
        fill_bias(bias_ref, text_len, video_len)

    for block in range(seq_len // BLOCK):
        rows = pl.ds(block * BLOCK, BLOCK)
        q_rows = q_ref[rows, :]
        d_rows = d_ref[rows, :]
        products = d_rows.astype(jnp.float32) * out_ref[rows, :].astype(jnp.float32)
        row_dots = jnp.sum(products.T, axis=0, keepdims=True)
        scores = dot(k_ref[...], q_rows, 1, 1) * (score_scale * LOG2E) + bias_ref[...]
        probs = jnp.exp2(scores - lse_ref[0, :, rows])
        d_probs = dot(v_ref[...], d_rows, 1, 1)
        d_scores = (probs * (d_probs - row_dots)).astype(jnp.bfloat16)
        v_part = dot(probs.astype(jnp.bfloat16), d_rows, 1, 0)
        k_part = dot(d_scores, q_rows, 1, 0)
        q_part = dot(k_ref[...], d_scores, 0, 0).T
        dq_ref[rows, :] = (q_part * score_scale).astype(jnp.bfloat16)
        if block == 0:
            dk_sum[...] = k_part
            dv_sum[...] = v_part
        else:
            dk_sum[...] += k_part
            dv_sum[...] += v_part
    dk_ref[...] = (dk_sum[...] * score_scale).astype(jnp.bfloat16)
    dv_ref[...] = dv_sum[...].astype(jnp.bfloat16)


def head_spec(seq_len, first):
    return pl.BlockSpec((seq_len, HD), lambda head: (0, first + head))


def attend(lens, tokens):
    seq_len, width = tokens.shape
    heads = width // (3 * HD)
    work = heads * seq_len * seq_len
    return pl.pallas_call(
        forward_kernel,
        grid=(heads,),
        in_specs=[pl.BlockSpec(memory_space=pltpu.SMEM)]
        + [head_spec(seq_len, member * heads) for member in range(3)],
        out_specs=[
            head_spec(seq_len, 0),
            pl.BlockSpec((1, 1, seq_len), lambda head: (head, 0, 0)),
        ],
        out_shape=[
            jax.ShapeDtypeStruct((seq_len, heads * HD), jnp.bfloat16),
            jax.ShapeDtypeStruct((heads, 1, seq_len), jnp.float32),
        ],
        scratch_shapes=[pltpu.VMEM((seq_len, BLOCK), jnp.float32)],
        compiler_params=pltpu.CompilerParams(dimension_semantics=("arbitrary",)),
        cost_estimate=pl.CostEstimate(
            flops=8 * HD * work, bytes_accessed=8 * seq_len * width // 3, transcendentals=2 * work
        ),
        name="attend",
    )(lens, tokens, tokens, tokens)


def attend_back(lens, tokens, results, d_results, log_totals):
    seq_len, width = tokens.shape
    heads = width // (3 * HD)
    work = heads * seq_len * seq_len
    gradient = jax.ShapeDtypeStruct((seq_len, heads * HD), jnp.bfloat16)
    return pl.pallas_call(
        backward_kernel,
        grid=(heads,),
        in_specs=[pl.BlockSpec(memory_space=pltpu.SMEM)]
        + [head_spec(seq_len, member * heads) for member in range(3)]
        + [
            head_spec(seq_len, 0),
            head_spec(seq_len, 0),
            pl.BlockSpec((1, 1, seq_len), lambda head: (head, 0, 0)),
        ],
        out_specs=[head_spec(seq_len, 0)] * 3,
        out_shape=[gradient] * 3,
        scratch_shapes=[
            pltpu.VMEM((seq_len, BLOCK), jnp.float32),
            pltpu.VMEM((seq_len, HD), jnp.float32),
            pltpu.VMEM((seq_len, HD), jnp.float32),
        ],
        compiler_params=pltpu.CompilerParams(dimension_semantics=("arbitrary",)),
        cost_estimate=pl.CostEstimate(
            flops=20 * HD * work, bytes_accessed=16 * seq_len * width // 3, transcendentals=work
        ),
        name="attend_back",
    )(lens, tokens, tokens, tokens, results, d_results, log_totals)


def swap(blocks, axis):
    return lax.all_to_all(blocks, axis, split_axis=0, concat_axis=0, tiled=True)


def regroup(rows, order):
    groups = lax.axis_size("dp")
    spread = swap(rows.reshape(groups, rows.shape[0] // groups, rows.shape[1]), "dp")
    return swap(jnp.take(spread, order, axis=0), "dp").reshape(rows.shape)


def body(qkv, gate, cotangent, out_weight, clip_lengths, text_lengths, plan):
    groups = lax.axis_size("dp")
    ways = lax.axis_size("seq")
    ordinal = jnp.arange(groups, dtype=jnp.int32)
    inverse = jnp.sum(jnp.where(plan[None, :] == ordinal[:, None], ordinal[None, :], 0), axis=1)
    home_clip = 2 * lax.axis_index("dp")
    head_width, model_width = out_weight.shape
    local_width = head_width // ways
    rows = cotangent.shape[1]
    seq_len = rows * ways
    slots = (1, 0)

    lens, tokens = {}, {}
    for slot in slots:
        lens[slot] = jnp.stack([text_lengths[home_clip + slot], clip_lengths[home_clip + slot]])
        parted = qkv[slot].reshape(rows, 3, ways, local_width).transpose(2, 0, 1, 3)
        parted = parted.reshape(ways, rows, 3 * local_width)
        tokens[slot] = swap(parted, "seq").reshape(seq_len, 3 * local_width)

    results, log_totals, attn = {}, {}, {}
    for slot in slots:
        results[slot], log_totals[slot] = attend(lens[slot], tokens[slot])
        back = swap(results[slot].reshape(ways, rows, local_width), "seq")
        attn[slot] = back.transpose(1, 0, 2).reshape(rows, head_width)
    attn[1] = regroup(attn[1], inverse)

    mixed, gate_parts, scaled, grads = {}, {}, {}, {}
    for slot in (0, 1):
        outputs = jnp.dot(attn[slot], out_weight, preferred_element_type=jnp.float32)
        arriving = cotangent[slot].astype(jnp.float32)
        mixed[slot] = (gate[slot][None, :] * outputs).astype(jnp.bfloat16)
        gate_parts[slot] = jnp.sum(arriving * outputs, axis=0)
        scaled[slot] = (arriving * gate[slot][None, :]).astype(jnp.bfloat16)
        d_attn = dot(scaled[slot], out_weight, 1, 1).astype(jnp.bfloat16)
        if slot == 1:
            d_attn = regroup(d_attn, plan)
        d_parted = d_attn.reshape(rows, ways, local_width).transpose(1, 0, 2)
        d_heads = swap(d_parted, "seq").reshape(seq_len, local_width)
        parts = attend_back(lens[slot], tokens[slot], results[slot], d_heads, log_totals[slot])
        leaving = jnp.concatenate(parts, axis=1).reshape(ways, rows, 3 * local_width)
        landed = swap(leaving, "seq").reshape(ways, rows, 3, local_width)
        grads[slot] = landed.transpose(1, 2, 0, 3).reshape(rows, 3 * head_width)

    partial_weight = dot(
        jnp.concatenate([attn[0], attn[1]]), jnp.concatenate([scaled[0], scaled[1]]), 0, 0
    ).astype(jnp.bfloat16)
    group_weight = lax.psum_scatter(partial_weight, "dp", scatter_dimension=1, tiled=True)
    column_parts = group_weight.reshape(head_width, ways, -1).transpose(1, 0, 2)
    weight_grad = jnp.sum(swap(column_parts, "seq").astype(jnp.float32), axis=0)

    gate_part = jnp.stack([gate_parts[0], gate_parts[1]])
    gate_all = swap(jnp.broadcast_to(gate_part[None], (ways,) + gate_part.shape), "seq")
    gate_grad = jnp.sum(gate_all, axis=0)
    return (
        jnp.stack([mixed[0], mixed[1]]),
        gate_grad,
        weight_grad,
        jnp.stack([grads[0], grads[1]]),
    )


def solution(mesh):
    in_specs = (P("dp", "seq", None), P("dp", None), P("dp", "seq", None), P(), P(), P(), P())
    out_specs = (P("dp", "seq", None), P("dp", None), P(None, ("dp", "seq")), P("dp", "seq", None))
    return jax.shard_map(body, mesh=mesh, in_specs=in_specs, out_specs=out_specs, check_vma=False)
```

profile of v0, /device:TPU:0, one launch (start us, length us, event | category | flops | bytes accessed | tf_op | source)
XLA Modules:
  0.0 525.0 jit_solution(789815775588060756)
XLA Ops:
  7.2 4.9 fusion.13
  16.4 6.5 %all-to-all-start.2 = ((bf16[4,256,1152]{1,2,0:T(8,128)(2,1)}), bf16[4,256,1152]{1,2,0:T(8,128)(2,1)S(1)}, u32[]{:S(2)}, u32[]{:S(2)}) async-start(bf16[4,256,1152]{1,2,0:T(8,128)(2,1)} %bitcast.69), calls=%async_computation.2 | async-start | bytes 4718592 | tf_op jit(solution)/shard_map/all_to_all | solution.py:152
  25.4 51.3 %all-to-all-done.2 = bf16[4,256,1152]{1,2,0:T(8,128)(2,1)S(1)} async-done(((bf16[4,256,1152]{1,2,0:T(8,128)(2,1)}), bf16[4,256,1152]{1,2,0:T(8,128)(2,1)S(1)}, u32[]{:S(2)}, u32[]{:S(2)}) %all-to-all-start.2) | async-done | bytes 2359328 | tf_op jit(solution)/shard_map/all_to_all | solution.py:152
  79.3 12.6 %attend.3 = (bf16[1024,384]{1,0:T(8,128)(2,1)}, f32[3,1,1024]{2,1,0:T(1,128)}) custom-call(s32[2]{0:T(128)} %pad_add_fusion.1.lens_ref, bf16[1024,1152]{1,0:T(8,128)(2,1)} %bitcast.85, bf16[1024,1152]{1,0:T(8,128)(2,1)} %bitcast.86, bf16[1024,1152]{1,0:T(8,128)(2,1)} %bitcast.87), custom_call_target="tpu_custom_call" | custom-call | flops 3221225472 | bytes 3145728 | tf_op jit(solution)/shard_map/attend/pallas_call | solution.py:99
  99.8 15.2 %all-to-all-done.3 = bf16[4,256,384]{2,1,0:T(8,128)(2,1)S(1)} async-done(((bf16[4,256,384]{2,1,0:T(8,128)(2,1)}), bf16[4,256,384]{2,1,0:T(8,128)(2,1)S(1)}, u32[]{:S(2)}, u32[]{:S(2)}) %all-to-all-start.3) | async-done | bytes 786464 | tf_op jit(solution)/shard_map/all_to_all | solution.py:152
  122.7 49.4 %all-to-all-done = bf16[4,256,1152]{1,2,0:T(8,128)(2,1)S(1)} async-done(((bf16[4,256,1152]{1,2,0:T(8,128)(2,1)}), bf16[4,256,1152]{1,2,0:T(8,128)(2,1)S(1)}, u32[]{:S(2)}, u32[]{:S(2)}) %all-to-all-start) | async-done | bytes 2359328 | tf_op jit(solution)/shard_map/all_to_all | solution.py:152
  180.1 12.7 %attend.2 = (bf16[1024,384]{1,0:T(8,128)(2,1)}, f32[3,1,1024]{2,1,0:T(1,128)}) custom-call(s32[2]{0:T(128)} %pad_add_fusion.lens_ref, bf16[1024,1152]{1,0:T(8,128)(2,1)} %bitcast.91, bf16[1024,1152]{1,0:T(8,128)(2,1)} %bitcast.92, bf16[1024,1152]{1,0:T(8,128)(2,1)} %bitcast.93), custom_call_target="tpu_custom_call" | custom-call | flops 3221225472 | bytes 3145728 | tf_op jit(solution)/shard_map/attend/pallas_call | solution.py:99
  200.2 19.3 %all-to-all-done.1 = bf16[4,256,384]{1,2,0:T(8,128)(2,1)S(1)} async-done(((bf16[4,256,384]{1,2,0:T(8,128)(2,1)}), bf16[4,256,384]{1,2,0:T(8,128)(2,1)S(1)}, u32[]{:S(2)}, u32[]{:S(2)}) %all-to-all-start.1) | async-done | bytes 786464 | tf_op jit(solution)/shard_map/all_to_all | solution.py:152
  223.6 8.0 %fusion.17 = f32[256,3072]{1,0:T(8,128)} fusion(bf16[256,1536]{0,1:T(8,128)(2,1)S(1)} %bitcast.79, bf16[1536,3072]{1,0:T(8,128)(2,1)} %param.12), kind=kOutput, calls=%fused_computation.47 | convolution fusion | flops 2415919104 | bytes 13369344 | tf_op jit(solution)/shard_map/dot_general | solution.py:189
  231.6 4.3 all-to-all-done.5
  236.2 9.8 %fusion.1 = (bf16[256,3072]{1,0:T(8,128)(2,1)S(1)}, bf16[256,3072]{1,0:T(8,128)(2,1)S(1)}, f32[3072]{0:T(1024)S(1)}, f32[3072]{0:T(1024)S(1)}, bf16[1,256,3072]{2,1,0:T(8,128)(2,1)}, /*index=5*/bf16[1,256,3072]{2,1,0:T(8,128)(2,1)}) fusion(f32[3072]{0:T(1024)S(1)} %bitcast.103, bf16[2,256,3072]{2,1,0:T(8,128)(2,1)} %param.11, f32[3072]{0:T(1024)S(1)} %bitcast.104, ...), kind=kOutput, calls=%fused_computation.9 | convolution fusion | flops 2426923008 | bytes 22855680 | tf_op jit(solution)/shard_map/dot_general | solution.py:189
  247.6 7.7 %convolution_convert_fusion = bf16[1536,3072]{1,0:T(8,128)(2,1)} fusion(bf16[256,3072]{1,0:T(8,128)(2,1)S(1)} %get-tuple-element.46, bf16[256,3072]{1,0:T(8,128)(2,1)S(1)} %get-tuple-element.45, bf16[256,1536]{0,1:T(8,128)(2,1)S(1)} %copy.86, bf16[256,1536]{0,1:T(8,128)(2,1)S(1)} %bitcast.80), kind=kOutput, calls=%fused_computation.2 | convolution fusion | flops 4845993984 | bytes 14155776 | tf_op jit(solution)/shard_map/dot_general | solution.py:18
  255.4 12.6 %copy.95 = bf16[1536,3072]{0,1:T(8,128)(2,1)} copy(bf16[1536,3072]{1,0:T(8,128)(2,1)} %convolution_convert_fusion) | data formatting | bytes 18874368
  269.4 8.2 %convolution_convert_fusion.1 = bf16[256,1536]{1,0:T(8,128)(2,1)} fusion(bf16[256,3072]{1,0:T(8,128)(2,1)S(1)} %copy-done.10, bf16[1536,3072]{1,0:T(8,128)(2,1)} %param.12), kind=kOutput, calls=%fused_computation.18 | convolution fusion | flops 2416312320 | bytes 11796480 | tf_op jit(solution)/shard_map/dot_general | solution.py:18
  281.3 12.4 %all-to-all-done.10 = bf16[8,32,1536]{2,1,0:T(8,128)(2,1)S(1)} async-done(((bf16[8,32,1536]{2,1,0:T(8,128)(2,1)}), bf16[8,32,1536]{2,1,0:T(8,128)(2,1)S(1)}, u32[]{:S(2)}, u32[]{:S(2)}) %all-to-all-start.10) | async-done | bytes 786464 | tf_op jit(solution)/shard_map/all_to_all | solution.py:152
  307.3 7.1 %convolution_convert_fusion.2 = bf16[256,1536]{1,0:T(8,128)(2,1)S(1)} fusion(bf16[256,3072]{1,0:T(8,128)(2,1)} %copy-done.8, bf16[1536,3072]{1,0:T(8,128)(2,1)} %param.12), kind=kOutput, calls=%fused_computation.19 | convolution fusion | flops 2416312320 | bytes 11796480 | tf_op jit(solution)/shard_map/dot_general | solution.py:18
  315.5 12.7 %all-to-all-done.11 = bf16[8,32,1536]{2,1,0:T(8,128)(2,1)S(1)} async-done(((bf16[8,32,1536]{2,1,0:T(8,128)(2,1)}), bf16[8,32,1536]{2,1,0:T(8,128)(2,1)S(1)}, u32[]{:S(2)}, u32[]{:S(2)}) %all-to-all-start.11) | async-done | bytes 786464 | tf_op jit(solution)/shard_map/all_to_all | solution.py:152
  332.9 16.3 %all-to-all-done.8 = bf16[4,256,384]{2,1,0:T(8,128)(2,1)S(1)} async-done(((bf16[4,256,384]{2,1,0:T(8,128)(2,1)}), bf16[4,256,384]{2,1,0:T(8,128)(2,1)S(1)}, u32[]{:S(2)}, u32[]{:S(2)}) %all-to-all-start.8) | async-done | bytes 786464 | tf_op jit(solution)/shard_map/all_to_all | solution.py:152
  352.7 10.5 %attend_back.2 = (bf16[1024,384]{1,0:T(8,128)(2,1)}, bf16[1024,384]{1,0:T(8,128)(2,1)}, bf16[1024,384]{1,0:T(8,128)(2,1)}) custom-call(s32[2]{0:T(128)} %pad_add_fusion.lens_ref, bf16[1024,1152]{1,0:T(8,128)(2,1)} %bitcast.94, bf16[1024,1152]{1,0:T(8,128)(2,1)} %bitcast.95, bf16[1024,1152]{1,0:T(8,128)(2,1)} %bitcast.96, ...), custom_call_target="tpu_custom_call" | custom-call | flops 8053063680 | bytes 6291456 | tf_op jit(solution)/shard_map/attend_back/pallas_call | solution.py:126
  375.0 10.4 %attend_back.3 = (bf16[1024,384]{1,0:T(8,128)(2,1)}, bf16[1024,384]{1,0:T(8,128)(2,1)}, bf16[1024,384]{1,0:T(8,128)(2,1)}) custom-call(s32[2]{0:T(128)} %pad_add_fusion.1.lens_ref, bf16[1024,1152]{1,0:T(8,128)(2,1)} %bitcast.88, bf16[1024,1152]{1,0:T(8,128)(2,1)} %bitcast.89, bf16[1024,1152]{1,0:T(8,128)(2,1)} %bitcast.90, ...), custom_call_target="tpu_custom_call" | custom-call | flops 8053063680 | bytes 6291456 | tf_op jit(solution)/shard_map/attend_back/pallas_call | solution.py:126
  392.9 35.4 %all-to-all-done.9 = bf16[4,256,1152]{1,2,0:T(8,128)(2,1)S(1)} async-done(((bf16[4,256,1152]{1,2,0:T(8,128)(2,1)}), bf16[4,256,1152]{1,2,0:T(8,128)(2,1)S(1)}, u32[]{:S(2)}, u32[]{:S(2)}) %all-to-all-start.9) | async-done | bytes 2359328 | tf_op jit(solution)/shard_map/all_to_all | solution.py:152
  428.4 57.8 %all_to_all.70 = bf16[4,256,1152]{1,2,0:T(8,128)(2,1)} all-to-all(bf16[4,256,1152]{1,2,0:T(8,128)(2,1)} %copy.92), channel_id=1, replica_groups=mesh['dp'=8,'seq'=4] {'seq'}, dimensions={0} | all-to-all | bytes 4718592 | tf_op jit(solution)/shard_map/all_to_all | solution.py:152
  499.5 6.6 %copy.94 = bf16[2,256,4608]{2,1,0:T(8,128)(2,1)} copy(bf16[2,256,4608]{1,2,0:T(8,128)(2,1)} %pad_maximum_fusion) | data formatting | bytes 9437184
  506.1 11.1 %all-to-all-done.7 = bf16[4,1536,96]{1,2,0:T(8,128)(2,1)S(1)} async-done(((bf16[4,1536,96]{1,2,0:T(8,128)(2,1)}), bf16[4,1536,96]{1,2,0:T(8,128)(2,1)S(1)}, u32[]{:S(2)}, u32[]{:S(2)}) %all-to-all-start.7) | async-done | bytes 1179680 | tf_op jit(solution)/shard_map/all_to_all | solution.py:152
  (80 shorter events, 107.7 us)
Async XLA Ops:
  16.4 6.5 %copy-start.5 = (s32[16]{0:T(128)S(1)}, s32[16]{0:T(128)}, u32[]{:S(2)}) copy-start(s32[16]{0:T(128)} %param.14) | copy-start | bytes 196
  16.4 6.5 %copy-start.6 = (s32[16]{0:T(128)S(1)}, s32[16]{0:T(128)}, u32[]{:S(2)}) copy-start(s32[16]{0:T(128)} %param.13) | copy-start | bytes 196
  16.4 60.3 %all-to-all-start.2 = ((bf16[4,256,1152]{1,2,0:T(8,128)(2,1)}), bf16[4,256,1152]{1,2,0:T(8,128)(2,1)S(1)}, u32[]{:S(2)}, u32[]{:S(2)}) async-start(bf16[4,256,1152]{1,2,0:T(8,128)(2,1)} %bitcast.69), calls=%async_computation.2 | async-start | bytes 4718592 | tf_op jit(solution)/shard_map/all_to_all | solution.py:152
  91.9 23.1 %all-to-all-start.3 = ((bf16[4,256,384]{2,1,0:T(8,128)(2,1)}), bf16[4,256,384]{2,1,0:T(8,128)(2,1)S(1)}, u32[]{:S(2)}, u32[]{:S(2)}) async-start(bf16[4,256,384]{2,1,0:T(8,128)(2,1)} %bitcast.98), calls=%async_computation.3 | async-start | bytes 1572864 | tf_op jit(solution)/shard_map/all_to_all | solution.py:152
  99.8 18.9 %copy-start.7 = (s32[8]{0:T(128)S(1)}, s32[8]{0:T(128)}, u32[]{:S(2)}) copy-start(s32[8]{0:T(128)} %param.15) | copy-start | bytes 100
  115.1 57.0 %all-to-all-start = ((bf16[4,256,1152]{1,2,0:T(8,128)(2,1)}), bf16[4,256,1152]{1,2,0:T(8,128)(2,1)S(1)}, u32[]{:S(2)}, u32[]{:S(2)}) async-start(bf16[4,256,1152]{1,2,0:T(8,128)(2,1)} %bitcast.72), calls=%async_computation | async-start | bytes 4718592 | tf_op jit(solution)/shard_map/all_to_all | solution.py:152
  172.0 23.0 %all-to-all-start.4 = ((bf16[8,32,1536]{2,1,0:T(8,128)(2,1)}), bf16[8,32,1536]{2,1,0:T(8,128)(2,1)S(1)}, u32[]{:S(2)}, u32[]{:S(2)}) async-start(bf16[8,32,1536]{2,1,0:T(8,128)(2,1)} %reshape_reshape.6), calls=%async_computation.4 | async-start | bytes 1572864 | tf_op jit(solution)/shard_map/all_to_all | solution.py:152
  192.7 5.8 %copy-start.4 = (f32[2,3072]{1,0:T(2,128)S(1)}, f32[2,3072]{1,0:T(2,128)}, u32[]{:S(2)}) copy-start(f32[2,3072]{1,0:T(2,128)} %param.10) | copy-start | bytes 73732
  195.0 24.5 %all-to-all-start.1 = ((bf16[4,256,384]{1,2,0:T(8,128)(2,1)}), bf16[4,256,384]{1,2,0:T(8,128)(2,1)S(1)}, u32[]{:S(2)}, u32[]{:S(2)}) async-start(bf16[4,256,384]{1,2,0:T(8,128)(2,1)} %copy.80), calls=%async_computation.1 | async-start | bytes 1572864 | tf_op jit(solution)/shard_map/all_to_all | solution.py:152
  219.6 16.4 %all-to-all-start.5 = ((bf16[8,32,1536]{2,1,0:T(8,128)(2,1)}), bf16[8,32,1536]{2,1,0:T(8,128)(2,1)S(1)}, u32[]{:S(2)}, u32[]{:S(2)}) async-start(bf16[8,32,1536]{2,1,0:T(8,128)(2,1)} %broadcast_select_fusion.1), calls=%async_computation.5 | async-start | bytes 1572864 | tf_op jit(solution)/shard_map/all_to_all | solution.py:152
  223.4 262.8 %reduce-scatter.4.cloned.1.call-start = ((), (), s32[]{:S(2)}) async-start(), calls=%async_computation.15 | async-start | bytes 10616832
  246.0 1.7 copy-start.9
  268.0 1.4 copy-start.10
  277.6 16.1 %all-to-all-start.10 = ((bf16[8,32,1536]{2,1,0:T(8,128)(2,1)}), bf16[8,32,1536]{2,1,0:T(8,128)(2,1)S(1)}, u32[]{:S(2)}, u32[]{:S(2)}) async-start(bf16[8,32,1536]{2,1,0:T(8,128)(2,1)} %bitcast.33), calls=%async_computation.10 | async-start | bytes 1572864 | tf_op jit(solution)/shard_map/all_to_all | solution.py:152
  294.4 9.1 %all-to-all-start.6 = ((f32[4,2,3072]{2,1,0:T(2,128)}), f32[4,2,3072]{2,1,0:T(2,128)S(1)}, u32[]{:S(2)}, u32[]{:S(2)}) async-start(f32[4,2,3072]{2,1,0:T(2,128)} %broadcast_in_dim.32), calls=%async_computation.6 | async-start | bytes 196608 | tf_op jit(solution)/shard_map/all_to_all | solution.py:152
  303.5 10.9 %copy-start.3 = (f32[4,2,3072]{2,1,0:T(2,128)}, f32[4,2,3072]{2,1,0:T(2,128)S(1)}, u32[]{:S(2)}) copy-start(f32[4,2,3072]{2,1,0:T(2,128)S(1)} %all-to-all-done.6) | copy-start | bytes 294916
  303.5 24.7 %all-to-all-start.11 = ((bf16[8,32,1536]{2,1,0:T(8,128)(2,1)}), bf16[8,32,1536]{2,1,0:T(8,128)(2,1)S(1)}, u32[]{:S(2)}, u32[]{:S(2)}) async-start(bf16[8,32,1536]{2,1,0:T(8,128)(2,1)} %broadcast_select_fusion), calls=%async_computation.11 | async-start | bytes 1572864 | tf_op jit(solution)/shard_map/all_to_all | solution.py:152
  328.2 21.0 %all-to-all-start.8 = ((bf16[4,256,384]{2,1,0:T(8,128)(2,1)}), bf16[4,256,384]{2,1,0:T(8,128)(2,1)S(1)}, u32[]{:S(2)}, u32[]{:S(2)}) async-start(bf16[4,256,384]{2,1,0:T(8,128)(2,1)} %bitcast.67), calls=%async_computation.8 | async-start | bytes 1572864 | tf_op jit(solution)/shard_map/all_to_all | solution.py:152
  349.2 3.5 copy-start.2
  349.2 22.2 %all-to-all-start.12 = ((bf16[4,256,384]{2,1,0:T(8,128)(2,1)}), bf16[4,256,384]{2,1,0:T(8,128)(2,1)S(1)}, u32[]{:S(2)}, u32[]{:S(2)}) async-start(bf16[4,256,384]{2,1,0:T(8,128)(2,1)} %copy.91), calls=%async_computation.12 | async-start | bytes 1572864 | tf_op jit(solution)/shard_map/all_to_all | solution.py:152
  371.4 3.6 copy-start.1
  371.4 57.0 %all-to-all-start.9 = ((bf16[4,256,1152]{1,2,0:T(8,128)(2,1)}), bf16[4,256,1152]{1,2,0:T(8,128)(2,1)S(1)}, u32[]{:S(2)}, u32[]{:S(2)}) async-start(bf16[4,256,1152]{1,2,0:T(8,128)(2,1)} %copy.89), calls=%async_computation.9 | async-start | bytes 4718592 | tf_op jit(solution)/shard_map/all_to_all | solution.py:152
  486.2 31.0 %all-to-all-start.7 = ((bf16[4,1536,96]{1,2,0:T(8,128)(2,1)}), bf16[4,1536,96]{1,2,0:T(8,128)(2,1)S(1)}, u32[]{:S(2)}, u32[]{:S(2)}) async-start(bf16[4,1536,96]{1,2,0:T(8,128)(2,1)} %bitcast.97), calls=%async_computation.7 | async-start | bytes 2359296 | tf_op jit(solution)/shard_map/all_to_all | solution.py:152
  495.1 1.7 copy-start
  (1 other events, 1.2 us)
Sparse Core Ops, SparseCore 0:
  268.2 82.4 reduce-scatter.3
where the time goes:
time: 527 us; the launch traced here: 525 us
  waiting for transfers between devices  236 us (45%)
  local copies, waits for them, and re-layouts  60.7 us (12%)
  blocking collectives  57.8 us (11%)
  starting transfers between devices  49.6 us (9%)
  Pallas kernels  46.2 us (9%)
  matrix products  40.9 us (8%)
  other arithmetic  19.9 us (4%)
  between operations  14.3 us (3%)
    all_to_all x13, waiting for transfers between devices, swap(): return lax.all_to_all(blocks, axis, split_axis=0, concat_axis=0, tiled=True)  236 us
    all_to_all x1, blocking collectives, swap(): return lax.all_to_all(blocks, axis, split_axis=0, concat_axis=0, tiled=True)  57.8 us
    all_to_all x13, starting transfers between devices, swap(): return lax.all_to_all(blocks, axis, split_axis=0, concat_axis=0, tiled=True)  49.4 us
    unnamed x26, local copies, waits for them, and re-layouts  29.5 us
    pallas_call x2, Pallas kernels, attend(): pl.pallas_call(forward_kernel, grid=(heads,), in_specs=[pl.BlockSpec(memo...  25.3 us
    dot_general x3, matrix products, dot(): lax.dot_general(left, right, (((left_dim,), (right_dim,)), ((), ())), pre...  23.1 us
    pallas_call x2, Pallas kernels, attend_back(): pl.pallas_call(backward_kernel, grid=(heads,), in_specs=[pl.BlockSpec(mem...  20.9 us
    dot_general x2, matrix products, body(): jnp.dot(attn[slot], out_weight, preferred_element_type=jnp.float32)  17.8 us
  transfers between devices with their start and end apart: 14, of which 12 were waited for; matrix products, arithmetic and copies ran while one was open for 14% of the time, Pallas kernels for 6%

commit v1 on v0

v1 whole, which is shorter than its diff:
```python
import functools
import math

import jax
import jax.numpy as jnp
from jax import lax
from jax.experimental import pallas as pl
from jax.experimental.pallas import tpu as pltpu
from jax.sharding import PartitionSpec as P

HD = 128
TXT = 256
BLOCK = 256
WIDE = 512
NEGATIVE = -1e30
LOG2E = math.log2(math.e)
MESH = pl.DeviceIdType.MESH


def dot(left, right, left_dim, right_dim):
    return lax.dot_general(
        left, right, (((left_dim,), (right_dim,)), ((), ())), preferred_element_type=jnp.float32
    )


def live_places(places, text_len, video_len):
    return (places < text_len) | ((places >= TXT) & (places < TXT + video_len))


def aligned(start, size, unit=128):
    return pl.ds(pl.multiple_of(start, unit), size)


def bit_of(index, bit):
    return (index // (1 << bit)) % 2


def rest_value(count, taken, bits):
    value = 0
    for bit in range(bits):
        if bit not in taken:
            value += (count % 2) << bit
            count //= 2
    return value


def block_kernel(
    groups, ways,
    clip_ref, text_ref, plan_ref, gate_ref, qkv_ref, cot_ref, w_hbm,
    mixed_ref, gate_out, weight_out, grad_ref,
    w, cot, scaled, tok, heads_d, flat_d, land_o, even_o,
    parts_d, spread_d, pick_d, home_d, parts_o, spread_o, pick_o, home_o,
    partial, near, mid, low, z_near, z_far, gate_all, bias, dk_sum, dv_sum,
    load_sem, own_sem, out_sem,
    in_send, in_recv, d_send, d_recv, o_send, o_recv, g_send, g_recv,
    dp_send, dp_recv, rs_send, rs_recv, zw_send, zw_recv, gate_send, gate_recv,
):
    group, place = lax.axis_index("dp"), lax.axis_index("seq")
    rows, model = cot.shape[1], cot.shape[2]
    width = flat_d.shape[2]
    local = width // ways
    heads = local // HD
    seq_len = rows * ways
    part = rows // groups
    dp_bits = groups.bit_length() - 1
    z_order = sorted(range(1, ways), key=lambda k: -min(k, ways - k))
    my_rows = aligned(place * rows, rows, rows)

    barrier = pltpu.get_barrier_semaphore()
    for k in range(1, ways):
        pl.semaphore_signal(
            barrier, inc=1, device_id={"seq": lax.rem(place + k, ways)}, device_id_type=MESH
        )
    for k in range(1, groups):
        pl.semaphore_signal(
            barrier, inc=1, device_id={"dp": lax.rem(group + k, groups)}, device_id_type=MESH
        )
    pl.semaphore_wait(barrier, ways + groups - 2)

    sent = []

    def start(copy):
        copy.start()
        sent.append(copy)

    def to_z(source, target, send, recv, k):
        return pltpu.make_async_remote_copy(
            source, target, send, recv, {"seq": lax.rem(place + k, ways)}, MESH
        )

    def qkv_copy(slot, member, k):
        peer = lax.rem(place + k, ways)
        return to_z(
            qkv_ref.at[slot, :, aligned(member * width + peer * local, local)],
            tok.at[slot, my_rows, pl.ds(member * local, local)],
            in_send.at[slot, member, k - 1], in_recv.at[slot, member, k - 1], k,
        )

    def qkv_own(slot, member):
        return pltpu.make_async_copy(
            qkv_ref.at[slot, :, aligned(member * width + place * local, local)],
            tok.at[slot, my_rows, pl.ds(member * local, local)],
            own_sem.at[slot, member],
        )

    def d_copy(slot, k):
        peer = lax.rem(place + k, ways)
        return to_z(
            flat_d.at[slot, :, aligned(peer * local, local)], heads_d.at[slot, my_rows, :],
            d_send.at[slot, k - 1], d_recv.at[slot, k - 1], k,
        )

    def d_own(slot):
        return pltpu.make_async_copy(
            flat_d.at[slot, :, aligned(place * local, local)], heads_d.at[slot, my_rows, :],
            own_sem.at[slot, 3],
        )

    def o_copy(slot, head, k):
        peer = lax.rem(place + k, ways)
        return to_z(
            heads_d.at[slot, aligned(peer * rows, rows, rows), aligned(head * HD, HD)],
            land_o.at[slot, :, aligned(place * local + head * HD, HD)],
            o_send.at[slot, head, k - 1], o_recv.at[slot, head, k - 1], k,
        )

    def o_own(slot):
        return pltpu.make_async_copy(
            heads_d.at[slot, my_rows, :], land_o.at[slot, :, aligned(place * local, local)],
            own_sem.at[slot, 4],
        )

    def grad_copy(slot, member, k):
        peer = lax.rem(place + k, ways)
        return to_z(
            tok.at[slot, aligned(peer * rows, rows, rows), pl.ds(member * local, local)],
            grad_ref.at[slot, :, aligned(member * width + place * local, local)],
            g_send.at[slot, member, k - 1], g_recv.at[slot, member, k - 1], k,
        )

    def grad_own(slot, member):
        return pltpu.make_async_copy(
            tok.at[slot, my_rows, pl.ds(member * local, local)],
            grad_ref.at[slot, :, aligned(member * width + place * local, local)],
            own_sem.at[slot, 5 + member],
        )

    def dp_copy(source, target, which, k):
        peer = lax.rem(group + k, groups)
        return pltpu.make_async_remote_copy(
            source.at[peer], target.at[group],
            dp_send.at[which, k - 1], dp_recv.at[which, k - 1], {"dp": peer}, MESH,
        )

    def spread_start(source, target, which):
        for k in range(1, groups):
            start(dp_copy(source, target, which, k))
        target[group] = source[group]

    def spread_wait(source, target, which):
        for k in range(1, groups):
            dp_copy(source, target, which, k).wait_recv()

    def split_rows(source, slot, target):
        for index in range(groups):
            piece = source[slot].astype(jnp.float32)[index * part:(index + 1) * part]
            target[index] = piece.astype(jnp.bfloat16)

    def merge_rows(source, target, slot):
        merged = source[...].astype(jnp.float32).reshape(rows, width)
        target[slot] = merged.astype(jnp.bfloat16)

    def scale_rows(slot):
        def step(index, carry):
            columns = aligned(index * WIDE, WIDE)
            values = cot[slot, :, columns].astype(jnp.float32) * gate_ref[slot:slot + 1, columns]
            scaled[slot, :, columns] = values.astype(jnp.bfloat16)
            return carry

        lax.fori_loop(0, model // WIDE, step, 0)

    def back_project(slot):
        def step(index, carry):
            columns = aligned(index * BLOCK, BLOCK, BLOCK)
            flat_d[slot, :, columns] = dot(scaled[slot], w[columns, :], 1, 1).astype(jnp.bfloat16)
            return carry

        lax.fori_loop(0, width // BLOCK, step, 0)

    def attend(slot):
        text_len, video_len = text_ref[2 * group + slot], clip_ref[2 * group + slot]
        scale = HD ** (-0.5)
        places = lax.broadcasted_iota(jnp.int32, bias.shape, 0)
        bias[...] = jnp.where(live_places(places, text_len, video_len), 0.0, NEGATIVE)

        def head_step(head, carry):
            columns = aligned(head * HD, HD)
            k_columns = aligned(local + head * HD, HD)
            v_columns = aligned(2 * local + head * HD, HD)

            def step(block, inner):
                span = aligned(block * BLOCK, BLOCK, BLOCK)
                q_rows, d_rows = tok[slot, span, columns], heads_d[slot, span, columns]
                keys, values = tok[slot, :, k_columns], tok[slot, :, v_columns]
                scores = dot(keys, q_rows, 1, 1) * (scale * LOG2E) + bias[...]
                peak = jnp.max(scores, axis=0, keepdims=True)
                weights = jnp.exp2(scores - peak)
                total = jnp.sum(weights, axis=0, keepdims=True)
                spots = block * BLOCK + lax.broadcasted_iota(jnp.int32, (1, BLOCK), 1)
                share = jnp.where(live_places(spots, text_len, video_len), 1.0 / total, 0.0)
                probs = weights * share
                probs_low = probs.astype(jnp.bfloat16)
                attended = dot(values, probs_low, 0, 0).T.astype(jnp.bfloat16)
                products = d_rows.astype(jnp.float32) * attended.astype(jnp.float32)
                row_dots = jnp.sum(products.T, axis=0, keepdims=True)
                d_probs = dot(values, d_rows, 1, 1)
                d_scores = (probs * (d_probs - row_dots)).astype(jnp.bfloat16)
                v_part = dot(probs_low, d_rows, 1, 0)
                k_part = dot(d_scores, q_rows, 1, 0)
                q_part = dot(keys, d_scores, 0, 0).T
                tok[slot, span, columns] = (q_part * scale).astype(jnp.bfloat16)
                heads_d[slot, span, columns] = attended

                @pl.when(block == 0)
                def _():
                    dk_sum[...] = k_part
                    dv_sum[...] = v_part

                @pl.when(block > 0)
                def _():
                    dk_sum[...] += k_part
                    dv_sum[...] += v_part

                return inner

            lax.fori_loop(0, seq_len // BLOCK, step, 0)
            tok[slot, :, k_columns] = (dk_sum[...] * scale).astype(jnp.bfloat16)
            tok[slot, :, v_columns] = dv_sum[...].astype(jnp.bfloat16)
            for k in z_order:
                o_copy(slot, head, k).start()
            return carry

        lax.fori_loop(0, heads, head_step, 0)
        o_own(slot).start()

    def o_wait(slot):
        o_own(slot).wait()
        for head in range(heads):
            for k in z_order:
                o_copy(slot, head, k).wait_recv()

    def qkv_start(slot):
        for member in range(3):
            for k in z_order:
                start(qkv_copy(slot, member, k))
            qkv_own(slot, member).start()

    def d_start(slot):
        for k in z_order:
            start(d_copy(slot, k))
        d_own(slot).start()

    def in_wait(slot):
        for member in range(3):
            qkv_own(slot, member).wait()
            for k in z_order:
                qkv_copy(slot, member, k).wait_recv()
        d_own(slot).wait()
        for k in z_order:
            d_copy(slot, k).wait_recv()

    def grad_start(slot, member):
        for k in z_order:
            start(grad_copy(slot, member, k))
        grad_own(slot, member).start()

    cot_load = pltpu.make_async_copy(cot_ref, cot, load_sem.at[0])
    w_load = pltpu.make_async_copy(w_hbm, w, load_sem.at[1])
    qkv_start(1)
    cot_load.start()
    w_load.start()
    cot_load.wait()
    scale_rows(1)
    w_load.wait()
    back_project(1)
    split_rows(flat_d, 1, parts_d)
    spread_start(parts_d, spread_d, 0)
    scale_rows(0)
    back_project(0)
    spread_wait(parts_d, spread_d, 0)
    for index in range(groups):
        pick_d[index] = spread_d[plan_ref[index]]
    spread_start(pick_d, home_d, 1)
    spread_wait(pick_d, home_d, 1)
    merge_rows(home_d, flat_d, 1)
    d_start(1)
    qkv_start(0)
    d_start(0)

    in_wait(1)
    attend(1)
    in_wait(0)
    attend(0)
    for member in range(3):
        grad_start(1, member)
    for member in range(2):
        grad_start(0, member)

    o_wait(1)
    split_rows(land_o, 1, parts_o)
    spread_start(parts_o, spread_o, 2)
    spread_wait(parts_o, spread_o, 2)
    for index in range(groups):
        origin = 0
        for other in range(groups):
            origin = jnp.where(plan_ref[other] == index, other, origin)
        pick_o[index] = spread_o[origin]
    spread_start(pick_o, home_o, 3)
    o_wait(0)
    spread_wait(pick_o, home_o, 3)
    merge_rows(home_o, even_o, 0)

    block_rows = model // groups
    per_step = max(1, 384 // block_rows)
    piece_rows = block_rows // ways

    def weight_step(index):
        columns = aligned(index * (per_step * block_rows), per_step * block_rows)
        value = dot(scaled[0, :, columns], land_o[0], 0, 0)
        value += dot(scaled[1, :, columns], even_o[0], 0, 0)
        for inner in range(per_step):
            for way in range(ways):
                first = (inner * ways + way) * piece_rows
                partial[index * per_step + inner, way] = (
                    value[first:first + piece_rows].astype(jnp.bfloat16)
                )

    halves = (pl.ds(0, width // 2), pl.ds(width // 2, width // 2))
    orders = (list(range(dp_bits)), [0] + list(range(dp_bits - 1, 0, -1)))
    stages = []
    count = 0
    for stage in range(dp_bits):
        entries = []
        for half in range(2):
            order = orders[half]
            taken = order[:stage + 1]
            bit = order[stage]
            kept = sum((bit_of(group, other) << other for other in order[:stage]), 0)
            for index in range(groups >> (stage + 1)):
                rest = rest_value(index, taken, dp_bits)
                given = kept + (1 - bit_of(group, bit)) * (1 << bit) + rest
                held = kept + bit_of(group, bit) * (1 << bit) + rest
                entries.append((half, bit, index, given, held, count))
                count += 1
        stages.append(entries)

    def landed(stage, index, columns):
        if stage == 0:
            return near.at[index, :, :, columns]
        if stage == 1:
            return mid.at[index, :, :, columns]
        first = sum(groups >> (other + 1) for other in range(2, stage))
        return low.at[first + index, :, :, columns]

    def rs_copy(stage, entry):
        half, bit, index, given, _, number = entry
        partner = group + (1 - 2 * bit_of(group, bit)) * (1 << bit)
        return pltpu.make_async_remote_copy(
            partial.at[given, :, :, halves[half]], landed(stage, index, halves[half]),
            rs_send.at[number], rs_recv.at[number], {"dp": partner}, MESH,
        )

    def rs_start(stage):
        for entry in stages[stage]:
            start(rs_copy(stage, entry))

    def rs_finish(stage):
        for entry in stages[stage]:
            rs_copy(stage, entry).wait_recv()
            half, _, index, _, held, _ = entry
            arrived = landed(stage, index, halves[half])

            def step(way, carry):
                value = partial[held, way, :, halves[half]].astype(jnp.float32)
                value += arrived[way].astype(jnp.float32)
                partial[held, way, :, halves[half]] = value.astype(jnp.bfloat16)
                return carry

            lax.fori_loop(0, ways, step, 0)

    steps = groups // per_step
    mine = bit_of(group, 0)
    if per_step == 1:
        def far_step(index, carry):
            weight_step(2 * index + (1 - mine))
            return carry

        def near_step(index, carry):
            weight_step(2 * index + mine)
            return carry

        lax.fori_loop(0, steps // 2, far_step, 0)
        rs_start(0)
        lax.fori_loop(0, steps // 2, near_step, 0)
    else:
        def any_step(index, carry):
            weight_step(index)
            return carry

        lax.fori_loop(0, steps, any_step, 0)
        rs_start(0)

    def project(slot, rows_ref, row_slot):
        def step(index, carry):
            columns = aligned(index * WIDE, WIDE)
            outputs = dot(rows_ref[row_slot], w[:, columns], 1, 0)
            arriving = cot[slot, :, columns].astype(jnp.float32)
            gate_all[place, slot:slot + 1, columns] = jnp.sum(
                arriving * outputs, axis=0, keepdims=True
            )
            gated = outputs * gate_ref[slot:slot + 1, columns]
            cot[slot, :, columns] = gated.astype(jnp.bfloat16)
            return carry

        lax.fori_loop(0, model // WIDE, step, 0)
        pltpu.make_async_copy(cot.at[slot], mixed_ref.at[slot], out_sem.at[slot]).start()

    def gate_copy(k):
        return to_z(
            gate_all.at[place], gate_all.at[place], gate_send.at[k - 1], gate_recv.at[k - 1], k
        )

    rs_finish(0)
    rs_start(1)
    project(0, land_o, 0)
    project(1, even_o, 0)
    rs_finish(1)
    for stage in range(2, dp_bits):
        rs_start(stage)
        rs_finish(stage)

    z_low = bit_of(place, 0)
    z_high = bit_of(place, 1)
    half_ways = ways // 2

    def near_copy(index):
        return pltpu.make_async_remote_copy(
            partial.at[group, 2 * index + (1 - z_low)], z_near.at[index],
            zw_send.at[index], zw_recv.at[index], {"seq": place + 1 - 2 * z_low}, MESH,
        )

    for index in range(half_ways):
        start(near_copy(index))
    grad_start(0, 2)
    for k in z_order:
        start(gate_copy(k))
    for index in range(half_ways):
        near_copy(index).wait_recv()
        held = 2 * index + z_low
        value = partial[group, held].astype(jnp.float32) + z_near[index].astype(jnp.float32)
        partial[group, held] = value.astype(jnp.bfloat16)
    far_copy = pltpu.make_async_remote_copy(
        partial.at[group, 2 * (1 - z_high) + z_low], z_far,
        zw_send.at[half_ways], zw_recv.at[half_ways], {"seq": place + 2 - 4 * z_high}, MESH,
    )
    start(far_copy)
    for k in z_order:
        gate_copy(k).wait_recv()
    gate_out[...] = jnp.sum(gate_all[...], axis=0)
    far_copy.wait_recv()
    weight_out[...] = partial[group, place].astype(jnp.float32) + z_far[...].astype(jnp.float32)

    for slot in (0, 1):
        pltpu.make_async_copy(cot.at[slot], mixed_ref.at[slot], out_sem.at[slot]).wait()
        for member in range(3):
            grad_own(slot, member).wait()
            for k in z_order:
                grad_copy(slot, member, k).wait_recv()
        for head in range(heads):
            for k in z_order:
                o_copy(slot, head, k).wait_send()
    for copy in sent:
        copy.wait_send()


def body(qkv, gate, cotangent, out_weight, clip_lengths, text_lengths, plan):
    groups, ways = lax.axis_size("dp"), lax.axis_size("seq")
    slots, rows, full = qkv.shape
    width, model = out_weight.shape
    local, heads = width // ways, width // ways // HD
    seq_len, part = rows * ways, rows // groups
    piece = model // groups // ways
    low = jnp.bfloat16
    dp_bits = groups.bit_length() - 1
    reduced = sum(2 * (groups >> (stage + 1)) for stage in range(dp_bits))
    late = max(1, sum(groups >> (stage + 1) for stage in range(2, dp_bits)))
    dma = pltpu.SemaphoreType.DMA
    split = pltpu.VMEM((groups, part, width), low)
    scratch = [
        pltpu.VMEM((width, model), low),
        pltpu.VMEM((slots, rows, model), low),
        pltpu.VMEM((slots, rows, model), low),
        pltpu.VMEM((slots, seq_len, 3 * local), low),
        pltpu.VMEM((slots, seq_len, local), low),
        pltpu.VMEM((slots, rows, width), low),
        pltpu.VMEM((slots, rows, width), low),
        pltpu.VMEM((1, rows, width), low),
    ] + [split] * 8 + [
        pltpu.VMEM((groups, ways, piece, width), low),
        pltpu.VMEM((groups // 2, ways, piece, width), low),
        pltpu.VMEM((groups // 4, ways, piece, width), low),
        pltpu.VMEM((late, ways, piece, width), low),
        pltpu.VMEM((ways // 2, piece, width), low),
        pltpu.VMEM((piece, width), low),
        pltpu.VMEM((ways, slots, model), jnp.float32),
        pltpu.VMEM((seq_len, BLOCK), jnp.float32),
        pltpu.VMEM((seq_len, HD), jnp.float32),
        pltpu.VMEM((seq_len, HD), jnp.float32),
        dma((2,)), dma((slots, 8)), dma((slots,)),
    ]
    for shape in (
        (slots, 3, ways - 1), (slots, ways - 1), (slots, heads, ways - 1), (slots, 3, ways - 1),
        (4, groups - 1), (reduced,), (ways // 2 + 1,), (ways - 1,),
    ):
        scratch += [dma(shape), dma(shape)]
    smem, vmem, anywhere = (
        pl.BlockSpec(memory_space=space) for space in (pltpu.SMEM, pltpu.VMEM, pl.ANY)
    )
    mixed, gate_grad, weight_rows, qkv_grad = pl.pallas_call(
        functools.partial(block_kernel, groups, ways),
        in_specs=[smem] * 3 + [vmem] + [anywhere] * 3,
        out_specs=[anywhere, vmem, vmem, anywhere],
        out_shape=[
            jax.ShapeDtypeStruct(cotangent.shape, low),
            jax.ShapeDtypeStruct(gate.shape, jnp.float32),
            jax.ShapeDtypeStruct((piece, width), jnp.float32),
            jax.ShapeDtypeStruct(qkv.shape, low),
        ],
        scratch_shapes=scratch,
        compiler_params=pltpu.CompilerParams(
            collective_id=0, has_side_effects=True, vmem_limit_bytes=67_000_000
        ),
        name="attention_half",
    )(clip_lengths, text_lengths, plan, gate, qkv, cotangent, out_weight)
    return mixed, gate_grad, weight_rows.T, qkv_grad


def solution(mesh):
    in_specs = (P("dp", "seq", None), P("dp", None), P("dp", "seq", None), P(), P(), P(), P())
    out_specs = (P("dp", "seq", None), P("dp", None), P(None, ("dp", "seq")), P("dp", "seq", None))
    return jax.shard_map(body, mesh=mesh, in_specs=in_specs, out_specs=out_specs, check_vma=False)
```

time: 527 us -> 305 us (0.58)
  Pallas kernels: 46.2 us -> 297 us
  waiting for transfers between devices: 236 us -> 0 us
  blocking collectives: 57.8 us -> 0 us
  local copies, waits for them, and re-layouts: 60.7 us -> 7.53 us
  starting transfers between devices: 49.6 us -> 0 us
  matrix products: 40.9 us -> 0 us
  other arithmetic: 19.9 us -> 0 us
  between operations: 14.3 us -> 0.67 us
    pallas_call x4 -> x1, Pallas kernels: 46.2 us -> 297 us  [body(): pl.pallas_call(functools.partial(block_kernel, groups, ways), in_specs=[s...]
    all_to_all x13 -> x0, waiting for transfers between devices: 236 us -> none  [swap(): return lax.all_to_all(blocks, axis, split_axis=0, concat_axis=0, tiled=True)]
    all_to_all x1 -> x0, blocking collectives: 57.8 us -> none  [swap(): return lax.all_to_all(blocks, axis, split_axis=0, concat_axis=0, tiled=True)]
    all_to_all x13 -> x0, starting transfers between devices: 49.4 us -> none  [swap(): return lax.all_to_all(blocks, axis, split_axis=0, concat_axis=0, tiled=True)]
    dot_general x5 -> x0, matrix products: 40.9 us -> none  [the longest x3 23.1 us: dot(): lax.dot_general(left, right, (((left_dim,), (right_dim,)), ((), ())), pre...]
    unnamed x26 -> x10, local copies, waits for them, and re-layouts: 29.5 us -> 7.53 us
    reshape x5 -> x0, local copies, waits for them, and re-layouts: 10.4 us -> none  [the longest x2 6.81 us: body(): jnp.concatenate(parts, axis=1).reshape(ways, rows, 3 * local_width)]
    another operation x5 -> x0, other arithmetic: 10.2 us -> none  [the longest x1 3.83 us: body(): jnp.stack([mixed[0], mixed[1]])]
  transfers between devices with their start and end apart: 14 -> 0, of which waited for: 12 -> 0; matrix products, arithmetic and copies ran while one was open for 14% -> 0% of each run, Pallas kernels for 6% -> 0%
where the time goes in v1:
time: 305 us
  Pallas kernels  297 us (97%)
  local copies, waits for them, and re-layouts  7.53 us (2%)
    pallas_call x1, Pallas kernels, body(): pl.pallas_call(functools.partial(block_kernel, groups, ways), in_specs=[s...  297 us
    unnamed x10, local copies, waits for them, and re-layouts  7.53 us

profile of v1, /device:TPU:0, one launch (start us, length us, event | category | flops | bytes accessed | tf_op | source)
XLA Modules:
  0.0 304.7 jit_solution(7437816723708787713)
XLA Ops:
  0.6 296.5 %attention_half.1 = (bf16[2,256,3072]{2,1,0:T(8,128)(2,1)}, f32[2,3072]{1,0:T(2,128)}, f32[96,1536]{1,0:T(8,128)}, bf16[2,256,4608]{2,1,0:T(8,128)(2,1)}) custom-call(s32[16]{0:T(128)} %clip_ref.1, s32[16]{0:T(128)} %text_ref.1, s32[8]{0:T(128)} %plan_ref.1, f32[2,3072]{1,0:T(2,128)} %gate_ref.1, bf16[2,256,4608]{2,1,0:T(8,128)(2,1)} %qkv_ref.1, ...), custom_call_target="tpu_custom_call" | custom-call | tf_op jit(solution)/shard_map/attention_half/pallas_call | solution.py:529
  297.2 0.0 copy-start.2
  297.2 0.0 copy-start.1
  297.2 0.0 copy-start
  297.2 3.9 %copy.15 = bf16[2,256,3072]{2,1,0:T(8,128)(2,1)} copy(bf16[2,256,3072]{2,1,0:T(8,128)(2,1)} %get-tuple-element.16) | data formatting | bytes 6291456
  301.1 0.0 copy-done.2
  301.1 0.6 copy.16
  301.7 0.0 copy-done.1
  301.7 0.8 copy.17
  302.5 0.0 copy-done
  302.5 2.2 copy.18
Async XLA Ops:
  297.2 3.9 %copy-start.2 = (f32[2,3072]{1,0:T(2,128)S(1)}, f32[2,3072]{1,0:T(2,128)}, u32[]{:S(2)}) copy-start(f32[2,3072]{1,0:T(2,128)} %get-tuple-element.17) | copy-start | bytes 73732
  297.2 4.5 %copy-start.1 = (f32[96,1536]{1,0:T(8,128)S(1)}, f32[96,1536]{1,0:T(8,128)}, u32[]{:S(2)}) copy-start(f32[96,1536]{1,0:T(8,128)} %get-tuple-element.10) | copy-start | bytes 1769476
  297.2 5.3 %copy-start = (bf16[2,256,4608]{2,1,0:T(8,128)(2,1)S(1)}, bf16[2,256,4608]{2,1,0:T(8,128)(2,1)}, u32[]{:S(2)}) copy-start(bf16[2,256,4608]{2,1,0:T(8,128)(2,1)} %get-tuple-element.19) | copy-start | bytes 14155780

commit v2 on v1

--- a/solution.py
+++ b/solution.py
@@ -47,11 +47,11 @@
 def block_kernel(
     groups, ways,
     clip_ref, text_ref, plan_ref, gate_ref, qkv_ref, cot_ref, w_hbm,
-    mixed_ref, gate_out, weight_out, grad_ref,
-    w, cot, scaled, tok, heads_d, flat_d, land_o, even_o,
-    parts_d, spread_d, pick_d, home_d, parts_o, spread_o, pick_o, home_o,
+    cot, gate_out, weight_out, grad_ref,
+    w, scaled, tok, heads_d, flat_d, land_o,
+    parts, spread, home,
     partial, near, mid, low, z_near, z_far, gate_all, bias, dk_sum, dv_sum,
-    load_sem, own_sem, out_sem,
+    load_sem, own_sem,
     in_send, in_recv, d_send, d_recv, o_send, o_recv, g_send, g_recv,
     dp_send, dp_recv, rs_send, rs_recv, zw_send, zw_recv, gate_send, gate_recv,
 ):
@@ -154,8 +154,12 @@
 
     def spread_start(source, target, which):
         for k in range(1, groups):
-            start(dp_copy(source, target, which, k))
+            dp_copy(source, target, which, k).start()
         target[group] = source[group]
+
+    def spread_sent(source, target, which):
+        for k in range(1, groups):
+            dp_copy(source, target, which, k).wait_send()
 
     def spread_wait(source, target, which):
         for k in range(1, groups):
@@ -202,7 +206,8 @@
                 span = aligned(block * BLOCK, BLOCK, BLOCK)
                 q_rows, d_rows = tok[slot, span, columns], heads_d[slot, span, columns]
                 keys, values = tok[slot, :, k_columns], tok[slot, :, v_columns]
-                scores = dot(keys, q_rows, 1, 1) * (scale * LOG2E) + bias[...]
+                wide_bias = jnp.concatenate([bias[...]] * (BLOCK // HD), axis=1)
+                scores = dot(keys, q_rows, 1, 1) * (scale * LOG2E) + wide_bias
                 peak = jnp.max(scores, axis=0, keepdims=True)
                 weights = jnp.exp2(scores - peak)
                 total = jnp.sum(weights, axis=0, keepdims=True)
@@ -257,7 +262,7 @@
 
     def d_start(slot):
         for k in z_order:
-            start(d_copy(slot, k))
+            d_copy(slot, k).start()
         d_own(slot).start()
 
     def in_wait(slot):
@@ -283,16 +288,17 @@
     scale_rows(1)
     w_load.wait()
     back_project(1)
-    split_rows(flat_d, 1, parts_d)
-    spread_start(parts_d, spread_d, 0)
+    split_rows(flat_d, 1, parts)
+    spread_start(parts, spread, 0)
     scale_rows(0)
     back_project(0)
-    spread_wait(parts_d, spread_d, 0)
+    spread_wait(parts, spread, 0)
+    spread_sent(parts, spread, 0)
     for index in range(groups):
-        pick_d[index] = spread_d[plan_ref[index]]
-    spread_start(pick_d, home_d, 1)
-    spread_wait(pick_d, home_d, 1)
-    merge_rows(home_d, flat_d, 1)
+        parts[index] = spread[plan_ref[index]]
+    spread_start(parts, home, 1)
+    spread_wait(parts, home, 1)
+    merge_rows(home, flat_d, 1)
     d_start(1)
     qkv_start(0)
     d_start(0)
@@ -303,22 +309,25 @@
     attend(0)
     for member in range(3):
         grad_start(1, member)
-    for member in range(2):
-        grad_start(0, member)
+    grad_start(0, 0)
 
     o_wait(1)
-    split_rows(land_o, 1, parts_o)
-    spread_start(parts_o, spread_o, 2)
-    spread_wait(parts_o, spread_o, 2)
+    spread_sent(parts, home, 1)
+    split_rows(land_o, 1, parts)
+    spread_start(parts, spread, 2)
+    spread_wait(parts, spread, 2)
+    spread_sent(parts, spread, 2)
     for index in range(groups):
         origin = 0
         for other in range(groups):
             origin = jnp.where(plan_ref[other] == index, other, origin)
-        pick_o[index] = spread_o[origin]
-    spread_start(pick_o, home_o, 3)
+        parts[index] = spread[origin]
+    spread_start(parts, home, 3)
     o_wait(0)
-    spread_wait(pick_o, home_o, 3)
-    merge_rows(home_o, even_o, 0)
+    spread_wait(parts, home, 3)
+    for k in z_order:
+        d_copy(0, k).wait_send()
+    merge_rows(home, flat_d, 0)
 
     block_rows = model // groups
     per_step = max(1, 384 // block_rows)
@@ -327,7 +336,7 @@
     def weight_step(index):
         columns = aligned(index * (per_step * block_rows), per_step * block_rows)
         value = dot(scaled[0, :, columns], land_o[0], 0, 0)
-        value += dot(scaled[1, :, columns], even_o[0], 0, 0)
+        value += dot(scaled[1, :, columns], flat_d[0], 0, 0)
         for inner in range(per_step):
             for way in range(ways):
                 first = (inner * ways + way) * piece_rows
@@ -415,7 +424,7 @@
             columns = aligned(index * WIDE, WIDE)
             outputs = dot(rows_ref[row_slot], w[:, columns], 1, 0)
             arriving = cot[slot, :, columns].astype(jnp.float32)
-            gate_all[place, slot:slot + 1, columns] = jnp.sum(
+            gate_all[0, slot:slot + 1, columns] = jnp.sum(
                 arriving * outputs, axis=0, keepdims=True
             )
             gated = outputs * gate_ref[slot:slot + 1, columns]
@@ -423,17 +432,17 @@
             return carry
 
         lax.fori_loop(0, model // WIDE, step, 0)
-        pltpu.make_async_copy(cot.at[slot], mixed_ref.at[slot], out_sem.at[slot]).start()
-
-    def gate_copy(k):
-        return to_z(
-            gate_all.at[place], gate_all.at[place], gate_send.at[k - 1], gate_recv.at[k - 1], k
+
+    def gate_copy(step, peer):
+        return pltpu.make_async_remote_copy(
+            gate_all.at[2 * step], gate_all.at[2 * step + 1],
+            gate_send.at[step], gate_recv.at[step], {"seq": peer}, MESH,
         )
 
     rs_finish(0)
     rs_start(1)
     project(0, land_o, 0)
-    project(1, even_o, 0)
+    project(1, flat_d, 0)
     rs_finish(1)
     for stage in range(2, dp_bits):
         rs_start(stage)
@@ -451,9 +460,9 @@
 
     for index in range(half_ways):
         start(near_copy(index))
-    grad_start(0, 2)
-    for k in z_order:
-        start(gate_copy(k))
+    grad_start(0, 1)
+    gate_near = gate_copy(0, place + 1 - 2 * z_low)
+    start(gate_near)
     for index in range(half_ways):
         near_copy(index).wait_recv()
         held = 2 * index + z_low
@@ -464,14 +473,17 @@
         zw_send.at[half_ways], zw_recv.at[half_ways], {"seq": place + 2 - 4 * z_high}, MESH,
     )
     start(far_copy)
-    for k in z_order:
-        gate_copy(k).wait_recv()
-    gate_out[...] = jnp.sum(gate_all[...], axis=0)
+    grad_start(0, 2)
+    gate_near.wait_recv()
+    gate_all[2] = gate_all[0] + gate_all[1]
+    gate_far = gate_copy(1, place + 2 - 4 * z_high)
+    start(gate_far)
+    gate_far.wait_recv()
+    gate_out[...] = gate_all[2] + gate_all[3]
     far_copy.wait_recv()
     weight_out[...] = partial[group, place].astype(jnp.float32) + z_far[...].astype(jnp.float32)
 
     for slot in (0, 1):
-        pltpu.make_async_copy(cot.at[slot], mixed_ref.at[slot], out_sem.at[slot]).wait()
         for member in range(3):
             grad_own(slot, member).wait()
             for k in z_order:
@@ -479,8 +491,36 @@
         for head in range(heads):
             for k in z_order:
                 o_copy(slot, head, k).wait_send()
+    spread_sent(parts, home, 3)
+    for k in z_order:
+        d_copy(1, k).wait_send()
     for copy in sent:
         copy.wait_send()
+
+
+def settle_kernel(*refs):
+    count = (len(refs) - 1) // 2
+    sources, targets, sems = refs[:count], refs[count:2 * count], refs[-1]
+    copies = [
+        pltpu.make_async_copy(source, target, sems.at[index])
+        for index, (source, target) in enumerate(zip(sources, targets))
+    ]
+    for copy in copies:
+        copy.start()
+    for copy in copies:
+        copy.wait()
+
+
+def settle(arrays):
+    return pl.pallas_call(
+        settle_kernel,
+        in_specs=[pl.BlockSpec(memory_space=pltpu.VMEM)] * len(arrays),
+        out_specs=[pl.BlockSpec(memory_space=pl.ANY)] * len(arrays),
+        out_shape=[jax.ShapeDtypeStruct(array.shape, array.dtype) for array in arrays],
+        scratch_shapes=[pltpu.SemaphoreType.DMA((len(arrays),))],
+        compiler_params=pltpu.CompilerParams(vmem_limit_bytes=2_000_000),
+        name="settle",
+    )(*arrays)
 
 
 def body(qkv, gate, cotangent, out_weight, clip_lengths, text_lengths, plan):
@@ -499,49 +539,48 @@
     scratch = [
         pltpu.VMEM((width, model), low),
         pltpu.VMEM((slots, rows, model), low),
-        pltpu.VMEM((slots, rows, model), low),
         pltpu.VMEM((slots, seq_len, 3 * local), low),
         pltpu.VMEM((slots, seq_len, local), low),
         pltpu.VMEM((slots, rows, width), low),
         pltpu.VMEM((slots, rows, width), low),
-        pltpu.VMEM((1, rows, width), low),
-    ] + [split] * 8 + [
+    ] + [split] * 3 + [
         pltpu.VMEM((groups, ways, piece, width), low),
         pltpu.VMEM((groups // 2, ways, piece, width), low),
         pltpu.VMEM((groups // 4, ways, piece, width), low),
         pltpu.VMEM((late, ways, piece, width), low),
         pltpu.VMEM((ways // 2, piece, width), low),
         pltpu.VMEM((piece, width), low),
-        pltpu.VMEM((ways, slots, model), jnp.float32),
-        pltpu.VMEM((seq_len, BLOCK), jnp.float32),
+        pltpu.VMEM((4, slots, model), jnp.float32),
         pltpu.VMEM((seq_len, HD), jnp.float32),
         pltpu.VMEM((seq_len, HD), jnp.float32),
-        dma((2,)), dma((slots, 8)), dma((slots,)),
+        pltpu.VMEM((seq_len, HD), jnp.float32),
+        dma((2,)), dma((slots, 8)),
     ]
     for shape in (
         (slots, 3, ways - 1), (slots, ways - 1), (slots, heads, ways - 1), (slots, 3, ways - 1),
-        (4, groups - 1), (reduced,), (ways // 2 + 1,), (ways - 1,),
+        (4, groups - 1), (reduced,), (ways // 2 + 1,), (2,),
     ):
         scratch += [dma(shape), dma(shape)]
     smem, vmem, anywhere = (
         pl.BlockSpec(memory_space=space) for space in (pltpu.SMEM, pltpu.VMEM, pl.ANY)
     )
-    mixed, gate_grad, weight_rows, qkv_grad = pl.pallas_call(
+    results = pl.pallas_call(
         functools.partial(block_kernel, groups, ways),
         in_specs=[smem] * 3 + [vmem] + [anywhere] * 3,
-        out_specs=[anywhere, vmem, vmem, anywhere],
+        out_specs=[vmem] * 4,
         out_shape=[
-            jax.ShapeDtypeStruct(cotangent.shape, low),
-            jax.ShapeDtypeStruct(gate.shape, jnp.float32),
-            jax.ShapeDtypeStruct((piece, width), jnp.float32),
-            jax.ShapeDtypeStruct(qkv.shape, low),
+            pltpu.VMEM(cotangent.shape, low),
+            pltpu.VMEM(gate.shape, jnp.float32),
+            pltpu.VMEM((piece, width), jnp.float32),
+            pltpu.VMEM(qkv.shape, low),
         ],
         scratch_shapes=scratch,
         compiler_params=pltpu.CompilerParams(
-            collective_id=0, has_side_effects=True, vmem_limit_bytes=67_000_000
+            collective_id=0, has_side_effects=True, vmem_limit_bytes=49_000_000
         ),
         name="attention_half",
     )(clip_lengths, text_lengths, plan, gate, qkv, cotangent, out_weight)
+    mixed, gate_grad, weight_rows, qkv_grad = settle(results)
     return mixed, gate_grad, weight_rows.T, qkv_grad
 
 

time: 305 us -> 299 us (0.980)
  local copies, waits for them, and re-layouts: 7.53 us -> 0 us
    unnamed x10 -> x0, local copies, waits for them, and re-layouts: 7.53 us -> none
    pallas_call x0 -> x1, Pallas kernels: none -> 3.46 us  [settle(): pl.pallas_call(settle_kernel, in_specs=[pl.BlockSpec(memory_space=pltpu.V...]
where the time goes in v2:
time: 299 us
  Pallas kernels  298 us (100%)
    pallas_call x1, Pallas kernels, body(): pl.pallas_call(functools.partial(block_kernel, groups, ways), in_specs=[s...  295 us

profile of v2, /device:TPU:0, one launch (start us, length us, event | category | flops | bytes accessed | tf_op | source)
XLA Modules:
  0.0 298.7 jit_solution(8685512006369021531)
XLA Ops:
  0.6 294.6 %attention_half.1 = (bf16[2,256,3072]{2,1,0:T(8,128)(2,1)S(1)}, f32[2,3072]{1,0:T(2,128)S(1)}, f32[96,1536]{1,0:T(8,128)S(1)}, bf16[2,256,4608]{2,1,0:T(8,128)(2,1)S(1)}) custom-call(s32[16]{0:T(128)} %clip_ref.1, s32[16]{0:T(128)} %text_ref.1, s32[8]{0:T(128)} %plan_ref.1, f32[2,3072]{1,0:T(2,128)} %gate_ref.1, bf16[2,256,4608]{2,1,0:T(8,128)(2,1)} %qkv_ref.1, ...), custom_call_target="tpu_custom_call" | custom-call | tf_op jit(solution)/shard_map/attention_half/pallas_call | solution.py:567
  295.2 3.5 %settle.1 = (bf16[2,256,3072]{2,1,0:T(8,128)(2,1)}, f32[2,3072]{1,0:T(2,128)}, f32[96,1536]{1,0:T(8,128)}, bf16[2,256,4608]{2,1,0:T(8,128)(2,1)}) custom-call(bf16[2,256,3072]{2,1,0:T(8,128)(2,1)S(1)} %get-tuple-element.12.refs_0_, f32[2,3072]{1,0:T(2,128)S(1)} %get-tuple-element.13.refs_1_, f32[96,1536]{1,0:T(8,128)S(1)} %get-tuple-element.14.refs_2_, ...), custom_call_target="tpu_custom_call" | custom-call | tf_op jit(solution)/shard_map/settle/pallas_call | solution.py:515

commit v3 on v2

--- a/solution.py
+++ b/solution.py
@@ -46,9 +46,9 @@
 
 def block_kernel(
     groups, ways,
-    clip_ref, text_ref, plan_ref, gate_ref, qkv_ref, cot_ref, w_hbm,
+    clip_hbm, text_hbm, plan_hbm, gate_hbm, qkv_ref, cot_ref, w_hbm,
     cot, gate_out, weight_out, grad_ref,
-    w, scaled, tok, heads_d, flat_d, land_o,
+    clip_ref, text_ref, plan_ref, w, gate_ref, scaled, tok, heads_d, flat_d, land_o,
     parts, spread, home,
     partial, near, mid, low, z_near, z_far, gate_all, bias, dk_sum, dv_sum,
     load_sem, own_sem,
@@ -281,9 +281,22 @@
 
     cot_load = pltpu.make_async_copy(cot_ref, cot, load_sem.at[0])
     w_load = pltpu.make_async_copy(w_hbm, w, load_sem.at[1])
+    gate_load = pltpu.make_async_copy(gate_hbm, gate_ref, load_sem.at[2])
     qkv_start(1)
+    tables = [
+        pltpu.make_async_copy(source, target, load_sem.at[3 + index])
+        for index, (source, target) in enumerate(
+            ((clip_hbm, clip_ref), (text_hbm, text_ref), (plan_hbm, plan_ref))
+        )
+    ]
+    for copy in tables:
+        copy.start()
+    gate_load.start()
     cot_load.start()
     w_load.start()
+    gate_load.wait()
+    for copy in tables:
+        copy.wait()
     cot_load.wait()
     scale_rows(1)
     w_load.wait()
@@ -537,7 +550,11 @@
     dma = pltpu.SemaphoreType.DMA
     split = pltpu.VMEM((groups, part, width), low)
     scratch = [
+        pltpu.SMEM(clip_lengths.shape, jnp.int32),
+        pltpu.SMEM(text_lengths.shape, jnp.int32),
+        pltpu.SMEM(plan.shape, jnp.int32),
         pltpu.VMEM((width, model), low),
+        pltpu.VMEM((slots, model), jnp.float32),
         pltpu.VMEM((slots, rows, model), low),
         pltpu.VMEM((slots, seq_len, 3 * local), low),
         pltpu.VMEM((slots, seq_len, local), low),
@@ -554,7 +571,7 @@
         pltpu.VMEM((seq_len, HD), jnp.float32),
         pltpu.VMEM((seq_len, HD), jnp.float32),
         pltpu.VMEM((seq_len, HD), jnp.float32),
-        dma((2,)), dma((slots, 8)),
+        dma((6,)), dma((slots, 8)),
     ]
     for shape in (
         (slots, 3, ways - 1), (slots, ways - 1), (slots, heads, ways - 1), (slots, 3, ways - 1),
@@ -566,7 +583,7 @@
     )
     results = pl.pallas_call(
         functools.partial(block_kernel, groups, ways),
-        in_specs=[smem] * 3 + [vmem] + [anywhere] * 3,
+        in_specs=[anywhere] * 7,
         out_specs=[vmem] * 4,
         out_shape=[
             pltpu.VMEM(cotangent.shape, low),

time: 299 us -> 298 us (level)
  no operation moved by 1% of the time
where the time goes in v3:
time: 298 us
  Pallas kernels  297 us (100%)
    pallas_call x1, Pallas kernels, body(): pl.pallas_call(functools.partial(block_kernel, groups, ways), in_specs=[a...  294 us

profile of v3, /device:TPU:0, one launch (start us, length us, event | category | flops | bytes accessed | tf_op | source)
XLA Modules:
  0.0 298.0 jit_solution(16845252335218930985)
XLA Ops:
  0.6 293.9 %attention_half.1 = (bf16[2,256,3072]{2,1,0:T(8,128)(2,1)S(1)}, f32[2,3072]{1,0:T(2,128)S(1)}, f32[96,1536]{1,0:T(8,128)S(1)}, bf16[2,256,4608]{2,1,0:T(8,128)(2,1)S(1)}) custom-call(s32[16]{0:T(128)} %clip_hbm.1, s32[16]{0:T(128)} %text_hbm.1, s32[8]{0:T(128)} %plan_hbm.1, f32[2,3072]{1,0:T(2,128)} %gate_hbm.1, bf16[2,256,4608]{2,1,0:T(8,128)(2,1)} %qkv_ref.1, ...), custom_call_target="tpu_custom_call" | custom-call | tf_op jit(solution)/shard_map/attention_half/pallas_call | solution.py:584
  294.5 3.5 %settle.1 = (bf16[2,256,3072]{2,1,0:T(8,128)(2,1)}, f32[2,3072]{1,0:T(2,128)}, f32[96,1536]{1,0:T(8,128)}, bf16[2,256,4608]{2,1,0:T(8,128)(2,1)}) custom-call(bf16[2,256,3072]{2,1,0:T(8,128)(2,1)S(1)} %get-tuple-element.12.refs_0_, f32[2,3072]{1,0:T(2,128)S(1)} %get-tuple-element.13.refs_1_, f32[96,1536]{1,0:T(8,128)S(1)} %get-tuple-element.14.refs_2_, ...), custom_call_target="tpu_custom_call" | custom-call | tf_op jit(solution)/shard_map/settle/pallas_call | solution.py:528
